TPU v7x, 32 devices: a whole 2x2x4 slice. The times are simulated.
32 devices in a mesh: head: 8 (over z, y), batch: 4 (over x, core).
Axes of the slice: x: 2, y: 2, z: 4, core: 2. Of those that a mesh axis runs over, the one named last changes fastest.
Arguments:
- incoming_hidden_stream: bfloat16 [512, 4096], P('batch'), may hold values from -6 to 6
- reception_projection: bfloat16 [4096, 4096], P(None, 'head'), may hold values from -0.09375 to 0.09375
- address_projection: bfloat16 [4096, 4096], P(None, 'head'), may hold values from -0.09375 to 0.09375
- payload_projection: bfloat16 [4096, 4096], P(None, 'head'), may hold values from -0.09375 to 0.09375
- sigmoid_filter_matrix: bfloat16 [4096, 4096], P(None, 'head'), may hold values from -0.09375 to 0.09375
- forgetting_speed: float32 [512, 4096], P('batch', 'head'), may hold values from 0.01 to 1.5
- adaptation_step_size: float32 [512, 4096], P('batch', 'head'), may hold values from 0 to 1
- diagonal_boost: float32 [4096], P('head'), may hold values from -0.6 to 0.6
- subspace_standardize_scale: float32 [4096], P('head'), may hold values from 0.5 to 2
- recurrent_memory_matrix: float32 [64, 64, 64, 64], P('batch', 'head'), may hold values from -6 to 6
- emission_projection: bfloat16 [4096, 4096], P('head'), may hold values from -0.09375 to 0.09375
- closing_standardize_scale: float32 [4096], replicated, may hold values from 0.7 to 2
- lexicon_projection: bfloat16 [4096, 65536], P(None, ('head', 'batch')), may hold values from -32 to 32
- proposed_tokens_list: int32 [64, 8], P('batch'), may hold values from 0 to 65535
- threshold_milli_nats: int32 [64, 8], P('batch'), may hold values from -22000 to -10001
Outputs:
- new_state: float32 [64, 64, 64, 64], P('batch', 'head')
- margin: float32 [64, 8], P('batch')
- accept: float32 [64, 8], P('batch')
All inputs are finite; a program needn't handle non-finite values.
Results may differ from a plain program's by a relative error of at most 0.0017.
Values may be sent and summed in bfloat16 or wider, within the bound.
No kernel may reach another device: no remote copies, remote signals or barrier semaphores. Data moves between devices by JAX's collectives and lax.ppermute only.
A program may use at most 128 MiB of HBM per device.

v0:
```python
import math
import jax
import jax.numpy as jnp
from jax import lax
from jax.sharding import PartitionSpec as P


def joined(x, axis, combine):
    everything = jax.tree.map(lambda part: lax.all_gather(part, axis), x)
    initial = jax.tree.map(lambda part: part[0], everything)

    def hop(k, so_far):
        return combine(so_far, jax.tree.map(lambda part: part[k], everything))

    return lax.fori_loop(1, lax.axis_size(axis), hop, initial)


def advance(start, reception_vectors, address_vectors, payload_vectors, decay, rate):
    unit = (
        address_vectors
        * lax.rsqrt(jnp.mean(address_vectors * address_vectors, -1, keepdims=True) + 1e-06)
        / math.sqrt(address_vectors.shape[-1])
    )
    inputs = tuple(
        (
            jnp.moveaxis(item, 1, 0)
            for item in (reception_vectors, address_vectors, payload_vectors, decay, unit, rate)
        )
    )

    def step(current, pieces):
        recept_now, keys_now, values_now, decay_now, unit_now, rate_now = pieces
        recall = jnp.einsum("bhij,bhj->bhi", current, unit_now, precision=lax.Precision.HIGHEST)
        current = (
            current * decay_now[:, :, None, :]
            - recall[:, :, :, None] * (unit_now * rate_now)[:, :, None, :]
            + values_now[:, :, :, None] * keys_now[:, :, None, :]
        )
        output = jnp.einsum("bhij,bhj->bhi", current, recept_now, precision=lax.Precision.HIGHEST)
        return (current, output)

    final, outputs = lax.scan(step, start, inputs)
    return (final, jnp.moveaxis(outputs, 0, 1))


def combine_stats(first, second):
    top = jnp.maximum(first[0], second[0])
    summed = first[1] * jnp.exp(first[0] - top) + second[1] * jnp.exp(second[0] - top)
    return (top, summed, first[2] + second[2])


def local_stats(logits, ids_flat, offset):
    peak = jnp.max(logits, -1)
    total = jnp.sum(jnp.exp(logits - peak[:, None]), -1)
    column = lax.broadcasted_iota(jnp.int32, logits.shape, 1)
    target = jnp.sum(jnp.where(column == (ids_flat - offset)[:, None], logits, 0.0), -1)
    return (peak, total, target)


def shards(
    incoming_hidden_stream,
    reception_projection,
    address_projection,
    payload_projection,
    sigmoid_filter_matrix,
    forgetting_speed,
    adaptation_step_size,
    diagonal_boost,
    subspace_standardize_scale,
    recurrent_memory_matrix,
    emission_projection,
    closing_standardize_scale,
    lexicon_projection,
    proposed_tokens_list,
    threshold_milli_nats,
):
    seq_dev, draft_len = proposed_tokens_list.shape
    lanes_on_shard, subspace_size = (
        recurrent_memory_matrix.shape[1],
        recurrent_memory_matrix.shape[2],
    )
    tok_dev = seq_dev * draft_len
    shape4 = (seq_dev, draft_len, lanes_on_shard, subspace_size)
    reception_vectors = jnp.dot(
        incoming_hidden_stream, reception_projection, preferred_element_type=jnp.float32
    ).reshape(shape4)
    address_vectors = jnp.dot(
        incoming_hidden_stream, address_projection, preferred_element_type=jnp.float32
    ).reshape(shape4)
    payload_vectors = jnp.dot(
        incoming_hidden_stream, payload_projection, preferred_element_type=jnp.float32
    ).reshape(shape4)
    gate = jnp.dot(
        incoming_hidden_stream, sigmoid_filter_matrix, preferred_element_type=jnp.float32
    )
    decay = jnp.exp(-forgetting_speed).reshape(shape4)
    rate = adaptation_step_size.reshape(shape4)
    new_state, wkv = advance(
        recurrent_memory_matrix, reception_vectors, address_vectors, payload_vectors, decay, rate
    )
    center = wkv - jnp.mean(wkv, -1, keepdims=True)
    interpolated_embedding = (
        center
        * lax.rsqrt(jnp.mean(center * center, -1, keepdims=True) + 1e-05)
        * subspace_standardize_scale.reshape(lanes_on_shard, subspace_size)
    )
    interpolated_embedding = (
        interpolated_embedding
        + jnp.sum(
            reception_vectors
            * address_vectors
            * diagonal_boost.reshape(lanes_on_shard, subspace_size),
            -1,
            keepdims=True,
        )
        * payload_vectors
    )
    gated = (
        interpolated_embedding.reshape(tok_dev, lanes_on_shard * subspace_size)
        * jax.nn.sigmoid(gate)
    ).astype(jnp.bfloat16)
    partial_out = jnp.dot(gated, emission_projection, preferred_element_type=jnp.float32)
    residual = incoming_hidden_stream.astype(jnp.float32) + lax.psum(partial_out, "head")
    centered = residual - jnp.mean(residual, -1, keepdims=True)
    normed = (
        centered
        * lax.rsqrt(jnp.mean(centered * centered, -1, keepdims=True) + 1e-05)
        * closing_standardize_scale
    ).astype(jnp.bfloat16)
    every, every_ids = (
        lax.all_gather(normed, "batch", axis=0, tiled=True),
        lax.all_gather(proposed_tokens_list, "batch", axis=0, tiled=True),
    )
    logits = jnp.dot(every, lexicon_projection, preferred_element_type=jnp.float32)
    vcols = lexicon_projection.shape[1]
    offset = (lax.axis_index("head") * lax.axis_size("batch") + lax.axis_index("batch")) * vcols
    peak, total, target = local_stats(logits, every_ids.reshape(-1), offset)
    peak, total, target = joined((peak, total, target), "batch", combine_stats)
    row_begin = lax.axis_index("batch") * tok_dev
    peak = lax.dynamic_slice_in_dim(peak, row_begin, tok_dev, 0)
    total = lax.dynamic_slice_in_dim(total, row_begin, tok_dev, 0)
    target = lax.dynamic_slice_in_dim(target, row_begin, tok_dev, 0)
    top = lax.pmax(peak, "head")
    summed, target = lax.psum((total * jnp.exp(peak - top), target), "head")
    logprob = target - (top + jnp.log(summed))
    margin = logprob.reshape(seq_dev, draft_len) - threshold_milli_nats.astype(jnp.float32) / 1000.0
    accept = jnp.cumprod(jax.nn.sigmoid(margin * 0.5), axis=1)
    return (new_state, margin, accept)


def solution(mesh):
    in_specs = (
        P("batch", None),
        P(None, "head"),
        P(None, "head"),
        P(None, "head"),
        P(None, "head"),
        P("batch", "head"),
        P("batch", "head"),
        P("head"),
        P("head"),
        P("batch", "head", None, None),
        P("head", None),
        P(),
        P(None, ("head", "batch")),
        P("batch", None),
        P("batch", None),
    )
    out_specs = (P("batch", "head", None, None), P("batch", None), P("batch", None))
    return jax.shard_map(shards, mesh=mesh, in_specs=in_specs, out_specs=out_specs, check_vma=False)
```

profile of v0, /device:TPU:0, one launch (start us, length us, event | category | flops | bytes accessed | tf_op | source)
XLA Modules:
  0.0 440.8 jit_solution(5631374826744188014)
XLA Ops:
  7.2 4.9 %copy.135 = f32[16,8,64,64]{3,2,1,0:T(8,128)} copy(f32[16,8,64,64]{3,2,1,0:T(8,128)} %param.28) | data formatting | bytes 4194304
  27.0 185.0 %while.31 = (s32[]{:T(128)}, f32[16,8,64,64]{3,2,1,0:T(8,128)}, f32[8,16,8,64]{3,2,1,0:T(8,128)S(1)}, f32[8,16,8,64]{3,2,0,1:T(8,128)S(1)}, f32[8,16,8,64]{3,2,1...) while((s32[]{:T(128)}, f32[16,8,64,64]{3,2,1,0:T(8,128)}, ...), condition=%wide.region_2.3_spmd, body=%wide.region_1.2_spmd.sunk | while | flops 15212546 | bytes 26017968 | solution.py:42
  28.0 8.6 %fusion.40 = f32[16,8,1,64]{3,2,1,0:T(1,128)S(1)} fusion(f32[16,8,64,1]{2,3,1,0:T(1,128)S(1)} %bitcast.112, f32[16,8,64,64]{3,2,1,0:T(8,128)} %get-tuple-element.464), kind=kOutput, calls=%fused_computation.53.clone.1 | convolution fusion | flops 6291456 | bytes 2162688 | tf_op jit(solution)/shard_map/while/body/eval_jaxpr/bhij,bhj->bhi/dot_general | solution.py:33
  38.4 3.1 multiply_add_fusion.5
  43.5 6.6 %fusion.41 = f32[16,8,1,64]{3,2,1,0:T(1,128)S(1)} fusion(f32[16,8,64,64]{3,2,1,0:T(8,128)S(1)} %multiply_add_fusion.5, f32[16,8,64,1]{2,3,1,0:T(1,128)S(1)} %bitcast.111), kind=kOutput, calls=%fused_computation.54.clone.1 | convolution fusion | flops 6291456 | bytes 2162688 | tf_op jit(solution)/shard_map/while/body/eval_jaxpr/bhij,bhj->bhi/dot_general | solution.py:39
  51.1 8.6 %fusion.40 = f32[16,8,1,64]{3,2,1,0:T(1,128)S(1)} fusion(f32[16,8,64,1]{2,3,1,0:T(1,128)S(1)} %bitcast.112, f32[16,8,64,64]{3,2,1,0:T(8,128)} %get-tuple-element.464), kind=kOutput, calls=%fused_computation.53.clone.1 | convolution fusion | flops 6291456 | bytes 2162688 | tf_op jit(solution)/shard_map/while/body/eval_jaxpr/bhij,bhj->bhi/dot_general | solution.py:33
  61.5 3.1 multiply_add_fusion.5
  66.6 6.6 %fusion.41 = f32[16,8,1,64]{3,2,1,0:T(1,128)S(1)} fusion(f32[16,8,64,64]{3,2,1,0:T(8,128)S(1)} %multiply_add_fusion.5, f32[16,8,64,1]{2,3,1,0:T(1,128)S(1)} %bitcast.111), kind=kOutput, calls=%fused_computation.54.clone.1 | convolution fusion | flops 6291456 | bytes 2162688 | tf_op jit(solution)/shard_map/while/body/eval_jaxpr/bhij,bhj->bhi/dot_general | solution.py:39
  74.3 8.6 %fusion.40 = f32[16,8,1,64]{3,2,1,0:T(1,128)S(1)} fusion(f32[16,8,64,1]{2,3,1,0:T(1,128)S(1)} %bitcast.112, f32[16,8,64,64]{3,2,1,0:T(8,128)} %get-tuple-element.464), kind=kOutput, calls=%fused_computation.53.clone.1 | convolution fusion | flops 6291456 | bytes 2162688 | tf_op jit(solution)/shard_map/while/body/eval_jaxpr/bhij,bhj->bhi/dot_general | solution.py:33
  84.6 3.1 multiply_add_fusion.5
  89.8 6.6 %fusion.41 = f32[16,8,1,64]{3,2,1,0:T(1,128)S(1)} fusion(f32[16,8,64,64]{3,2,1,0:T(8,128)S(1)} %multiply_add_fusion.5, f32[16,8,64,1]{2,3,1,0:T(1,128)S(1)} %bitcast.111), kind=kOutput, calls=%fused_computation.54.clone.1 | convolution fusion | flops 6291456 | bytes 2162688 | tf_op jit(solution)/shard_map/while/body/eval_jaxpr/bhij,bhj->bhi/dot_general | solution.py:39
  97.4 8.6 %fusion.40 = f32[16,8,1,64]{3,2,1,0:T(1,128)S(1)} fusion(f32[16,8,64,1]{2,3,1,0:T(1,128)S(1)} %bitcast.112, f32[16,8,64,64]{3,2,1,0:T(8,128)} %get-tuple-element.464), kind=kOutput, calls=%fused_computation.53.clone.1 | convolution fusion | flops 6291456 | bytes 2162688 | tf_op jit(solution)/shard_map/while/body/eval_jaxpr/bhij,bhj->bhi/dot_general | solution.py:33
  107.8 3.1 multiply_add_fusion.5
  112.9 6.6 %fusion.41 = f32[16,8,1,64]{3,2,1,0:T(1,128)S(1)} fusion(f32[16,8,64,64]{3,2,1,0:T(8,128)S(1)} %multiply_add_fusion.5, f32[16,8,64,1]{2,3,1,0:T(1,128)S(1)} %bitcast.111), kind=kOutput, calls=%fused_computation.54.clone.1 | convolution fusion | flops 6291456 | bytes 2162688 | tf_op jit(solution)/shard_map/while/body/eval_jaxpr/bhij,bhj->bhi/dot_general | solution.py:39
  120.5 8.6 %fusion.40 = f32[16,8,1,64]{3,2,1,0:T(1,128)S(1)} fusion(f32[16,8,64,1]{2,3,1,0:T(1,128)S(1)} %bitcast.112, f32[16,8,64,64]{3,2,1,0:T(8,128)} %get-tuple-element.464), kind=kOutput, calls=%fused_computation.53.clone.1 | convolution fusion | flops 6291456 | bytes 2162688 | tf_op jit(solution)/shard_map/while/body/eval_jaxpr/bhij,bhj->bhi/dot_general | solution.py:33
  136.0 6.6 %fusion.41 = f32[16,8,1,64]{3,2,1,0:T(1,128)S(1)} fusion(f32[16,8,64,64]{3,2,1,0:T(8,128)S(1)} %multiply_add_fusion.5, f32[16,8,64,1]{2,3,1,0:T(1,128)S(1)} %bitcast.111), kind=kOutput, calls=%fused_computation.54.clone.1 | convolution fusion | flops 6291456 | bytes 2162688 | tf_op jit(solution)/shard_map/while/body/eval_jaxpr/bhij,bhj->bhi/dot_general | solution.py:39
  143.7 8.6 %fusion.40 = f32[16,8,1,64]{3,2,1,0:T(1,128)S(1)} fusion(f32[16,8,64,1]{2,3,1,0:T(1,128)S(1)} %bitcast.112, f32[16,8,64,64]{3,2,1,0:T(8,128)} %get-tuple-element.464), kind=kOutput, calls=%fused_computation.53.clone.1 | convolution fusion | flops 6291456 | bytes 2162688 | tf_op jit(solution)/shard_map/while/body/eval_jaxpr/bhij,bhj->bhi/dot_general | solution.py:33
  159.1 6.6 %fusion.41 = f32[16,8,1,64]{3,2,1,0:T(1,128)S(1)} fusion(f32[16,8,64,64]{3,2,1,0:T(8,128)S(1)} %multiply_add_fusion.5, f32[16,8,64,1]{2,3,1,0:T(1,128)S(1)} %bitcast.111), kind=kOutput, calls=%fused_computation.54.clone.1 | convolution fusion | flops 6291456 | bytes 2162688 | tf_op jit(solution)/shard_map/while/body/eval_jaxpr/bhij,bhj->bhi/dot_general | solution.py:39
  166.8 8.6 %fusion.40 = f32[16,8,1,64]{3,2,1,0:T(1,128)S(1)} fusion(f32[16,8,64,1]{2,3,1,0:T(1,128)S(1)} %bitcast.112, f32[16,8,64,64]{3,2,1,0:T(8,128)} %get-tuple-element.464), kind=kOutput, calls=%fused_computation.53.clone.1 | convolution fusion | flops 6291456 | bytes 2162688 | tf_op jit(solution)/shard_map/while/body/eval_jaxpr/bhij,bhj->bhi/dot_general | solution.py:33
  182.3 6.6 %fusion.41 = f32[16,8,1,64]{3,2,1,0:T(1,128)S(1)} fusion(f32[16,8,64,64]{3,2,1,0:T(8,128)S(1)} %multiply_add_fusion.5, f32[16,8,64,1]{2,3,1,0:T(1,128)S(1)} %bitcast.111), kind=kOutput, calls=%fused_computation.54.clone.1 | convolution fusion | flops 6291456 | bytes 2162688 | tf_op jit(solution)/shard_map/while/body/eval_jaxpr/bhij,bhj->bhi/dot_general | solution.py:39
  189.9 8.6 %fusion.40 = f32[16,8,1,64]{3,2,1,0:T(1,128)S(1)} fusion(f32[16,8,64,1]{2,3,1,0:T(1,128)S(1)} %bitcast.112, f32[16,8,64,64]{3,2,1,0:T(8,128)} %get-tuple-element.464), kind=kOutput, calls=%fused_computation.53.clone.1 | convolution fusion | flops 6291456 | bytes 2162688 | tf_op jit(solution)/shard_map/while/body/eval_jaxpr/bhij,bhj->bhi/dot_general | solution.py:33
  205.4 6.6 %fusion.41 = f32[16,8,1,64]{3,2,1,0:T(1,128)S(1)} fusion(f32[16,8,64,64]{3,2,1,0:T(8,128)S(1)} %multiply_add_fusion.5, f32[16,8,64,1]{2,3,1,0:T(1,128)S(1)} %bitcast.111), kind=kOutput, calls=%fused_computation.54.clone.1 | convolution fusion | flops 6291456 | bytes 2162688 | tf_op jit(solution)/shard_map/while/body/eval_jaxpr/bhij,bhj->bhi/dot_general | solution.py:39
  213.8 6.2 %fusion.5 = f32[128,4096]{1,0:T(8,128)} fusion(bf16[512,4096]{1,0:T(8,128)(2,1)} %param.29, f32[128,512]{1,0:T(8,128)S(1)} %reshape.93, bf16[128,4096]{1,0:T(8,128)(2,1)S(1)} %copy-done.2, bf16[4096,512]{1,0:T(8,128)(2,1)} %param.23), kind=kOutput, calls=%fused_computation.24 | convolution fusion | flops 1074069504 | bytes 11796480 | tf_op jit(solution)/shard_map/dot_general | solution.py:122
  220.1 105.1 %all-reduce.3.cloned.1.call-done = f32[128,4096]{1,0:T(8,128)} async-done(((f32[128,4096]{1,0:T(8,128)}), f32[128,4096]{1,0:T(8,128)}) %all-reduce.3.cloned.1.call-update) | async-done | bytes 2097168 | tf_op jit(solution)/shard_map/psum | solution.py:123
  329.4 5.2 %all-gather.5 = s32[4,16,8]{1,2,0:T(8,128)S(1)} all-gather(s32[1,16,8]{1,2,0:T(8,128)S(1)} %bitcast.127), channel_id=1, replica_groups=mesh['head'=8,'batch'=4] {'batch'}, dimensions={0}, use_global_device_ids=true | all-gather | bytes 2560 | tf_op jit(solution)/shard_map/all_gather | solution.py:132
  334.9 28.4 %all-gather.9.cloned.1.call-done = bf16[512,4096]{1,0:T(8,128)(2,1)} async-done(((bf16[128,4096]{1,0:T(8,128)(2,1)}), bf16[512,4096]{1,0:T(8,128)(2,1)}) %all-gather.9.cloned.1.call-update) | async-done | bytes 4194320 | tf_op jit(solution)/shard_map/all_gather | solution.py:131
  363.3 13.1 %fusion.9 = (f32[512]{0:T(512)S(1)}, f32[512,2048]{1,0:T(8,128)S(1)}) fusion(bf16[512,4096]{1,0:T(8,128)(2,1)} %all-gather.9.cloned.1.call-done, bf16[4096,2048]{1,0:T(8,128)(2,1)} %param.31), kind=kOutput, calls=%fused_computation.52 | convolution fusion | flops 8590983168 | bytes 25167872 | tf_op jit(solution)/shard_map/dot_general | solution.py:134
  377.9 5.2 %all-gather.4 = f32[4,1,512]{2,1,0:T(1,128)S(1)} all-gather(f32[1,1,512]{2,1,0:T(1,128)S(1)} %bitcast.126), channel_id=3, replica_groups=mesh['head'=8,'batch'=4] {'batch'}, dimensions={0}, use_global_device_ids=true | all-gather | bytes 10240 | tf_op jit(solution)/shard_map/all_gather | solution.py:9
  383.1 5.2 %all-gather.6 = f32[4,1,512]{2,1,0:T(1,128)S(1)} all-gather(f32[1,1,512]{2,1,0:T(1,128)S(1)} %bitcast.125), channel_id=4, replica_groups=mesh['head'=8,'batch'=4] {'batch'}, dimensions={0}, use_global_device_ids=true | all-gather | bytes 10240 | tf_op jit(solution)/shard_map/all_gather | solution.py:9
  388.2 5.2 %all-gather.3 = f32[4,1,512]{2,1,0:T(1,128)S(1)} all-gather(f32[1,1,512]{2,1,0:T(1,128)S(1)} %bitcast.124), channel_id=2, replica_groups=mesh['head'=8,'batch'=4] {'batch'}, dimensions={0}, use_global_device_ids=true | all-gather | bytes 10240 | tf_op jit(solution)/shard_map/all_gather | solution.py:9
  393.7 21.3 %pmax.7 = f32[128]{0:T(128)S(1)} all-reduce(f32[128]{0:T(128)S(1)} %dynamic_slice.59), channel_id=1, replica_groups=mesh['head'=8,'batch'=4] {'head'}, use_global_device_ids=true, to_apply=%region_15.16 | all-reduce | flops 128 | bytes 1024 | tf_op jit(solution)/shard_map/pmax | solution.py:143
  415.2 17.1 %all-reduce = (f32[128]{0:T(128)S(1)}, f32[128]{0:T(128)S(1)}) all-reduce(f32[128]{0:T(128)S(1)} %dynamic_slice.58, f32[128]{0:T(128)S(1)} %exponential_multiply_fusion), channel_id=1, replica_groups=mesh['head'=8,'batch'=4] {'head'}, use_global_device_ids=true, to_apply=%region_14.15 | all-reduce | flops 256 | bytes 2048 | tf_op jit(solution)/shard_map/psum | solution.py:144
  (162 shorter events, 75.5 us)
Async XLA Ops:
  7.2 4.9 %copy-start.2 = (bf16[128,4096]{1,0:T(8,128)(2,1)S(1)}, bf16[128,4096]{1,0:T(8,128)(2,1)}, u32[]{:S(2)}) copy-start(bf16[128,4096]{1,0:T(8,128)(2,1)} %param.19) | copy-start | bytes 3145732
  7.2 318.0 %all-reduce.3.cloned.1.call-start = ((), (), s32[]{:S(2)}) async-start(), calls=%async_computation | async-start | bytes 4194304 | tf_op jit(solution)/shard_map/psum | solution.py:123
  15.0 3.2 copy-start.7
  27.0 186.0 %copy-start.8 = (f32[512]{0:T(512)S(1)}, f32[512]{0:T(512)}, u32[]{:S(2)}) copy-start(f32[512]{0:T(512)} %param.27) | copy-start | bytes 6148
  27.0 11.4 %copy-start = (f32[16,8,64,64]{3,2,1,0:T(8,128)S(1)}, f32[16,8,64,64]{3,2,1,0:T(8,128)}, u32[]{:S(2)}) copy-start(f32[16,8,64,64]{3,2,1,0:T(8,128)} %get-tuple-element.464) | copy-start | bytes 6291460 | tf_op jit(solution)/shard_map/while
  41.5 2.0 copy-start.1
  50.1 11.4 %copy-start = (f32[16,8,64,64]{3,2,1,0:T(8,128)S(1)}, f32[16,8,64,64]{3,2,1,0:T(8,128)}, u32[]{:S(2)}) copy-start(f32[16,8,64,64]{3,2,1,0:T(8,128)} %get-tuple-element.464) | copy-start | bytes 6291460 | tf_op jit(solution)/shard_map/while
  64.6 2.0 copy-start.1
  73.2 11.4 %copy-start = (f32[16,8,64,64]{3,2,1,0:T(8,128)S(1)}, f32[16,8,64,64]{3,2,1,0:T(8,128)}, u32[]{:S(2)}) copy-start(f32[16,8,64,64]{3,2,1,0:T(8,128)} %get-tuple-element.464) | copy-start | bytes 6291460 | tf_op jit(solution)/shard_map/while
  87.7 2.0 copy-start.1
  96.4 11.4 %copy-start = (f32[16,8,64,64]{3,2,1,0:T(8,128)S(1)}, f32[16,8,64,64]{3,2,1,0:T(8,128)}, u32[]{:S(2)}) copy-start(f32[16,8,64,64]{3,2,1,0:T(8,128)} %get-tuple-element.464) | copy-start | bytes 6291460 | tf_op jit(solution)/shard_map/while
  110.9 2.0 copy-start.1
  119.5 11.4 %copy-start = (f32[16,8,64,64]{3,2,1,0:T(8,128)S(1)}, f32[16,8,64,64]{3,2,1,0:T(8,128)}, u32[]{:S(2)}) copy-start(f32[16,8,64,64]{3,2,1,0:T(8,128)} %get-tuple-element.464) | copy-start | bytes 6291460 | tf_op jit(solution)/shard_map/while
  134.0 2.0 copy-start.1
  142.6 11.4 %copy-start = (f32[16,8,64,64]{3,2,1,0:T(8,128)S(1)}, f32[16,8,64,64]{3,2,1,0:T(8,128)}, u32[]{:S(2)}) copy-start(f32[16,8,64,64]{3,2,1,0:T(8,128)} %get-tuple-element.464) | copy-start | bytes 6291460 | tf_op jit(solution)/shard_map/while
  157.1 2.0 copy-start.1
  165.8 11.4 %copy-start = (f32[16,8,64,64]{3,2,1,0:T(8,128)S(1)}, f32[16,8,64,64]{3,2,1,0:T(8,128)}, u32[]{:S(2)}) copy-start(f32[16,8,64,64]{3,2,1,0:T(8,128)} %get-tuple-element.464) | copy-start | bytes 6291460 | tf_op jit(solution)/shard_map/while
  180.3 2.0 copy-start.1
  188.9 11.4 %copy-start = (f32[16,8,64,64]{3,2,1,0:T(8,128)S(1)}, f32[16,8,64,64]{3,2,1,0:T(8,128)}, u32[]{:S(2)}) copy-start(f32[16,8,64,64]{3,2,1,0:T(8,128)} %get-tuple-element.464) | copy-start | bytes 6291460 | tf_op jit(solution)/shard_map/while
  203.4 2.0 copy-start.1
  220.0 107.9 %copy-start.4 = (f32[4096]{0:T(1024)S(1)}, f32[4096]{0:T(1024)}, u32[]{:S(2)}) copy-start(f32[4096]{0:T(1024)} %param.30) | copy-start | bytes 49156
  220.0 143.3 %all-gather.9.cloned.1.call-start = ((), (), s32[]{:S(2)}) async-start(), calls=%async_computation.1 | async-start | bytes 5242880 | tf_op jit(solution)/shard_map/all_gather | solution.py:131
  325.2 2.2 copy-start.3
  327.4 2.0 copy-start.5
  327.4 7.4 %copy-start.6 = (s32[16,8]{0,1:T(8,128)S(1)}, s32[16,8]{0,1:T(8,128)}, u32[]{:S(2)}) copy-start(s32[16,8]{0,1:T(8,128)} %param.33) | copy-start | bytes 1540
Sparse Core Ops, SparseCore 0:
  220.1 105.0 all-reduce.2
  329.5 33.7 all-gather.8
where the time goes:
time: 442 us; the launch traced here: 441 us
  matrix products  149 us (34%)
  waiting for transfers between devices  134 us (30%)
  blocking collectives  59.2 us (13%)
  local copies, waits for them, and re-layouts  42.9 us (10%)
  other arithmetic  40.8 us (9%)
  between operations  14.3 us (3%)
    psum x1, waiting for transfers between devices, shards(): lax.psum(partial_out, 'head')  105 us
    dot_general x8, matrix products, step(): jnp.einsum('bhij,bhj->bhi', current, unit_now, precision=lax.Precision.HI...  68.7 us
    dot_general x8, matrix products, step(): jnp.einsum('bhij,bhj->bhi', current, recept_now, precision=lax.Precision....  52.6 us
    all_gather x1, waiting for transfers between devices, shards(): lax.all_gather(normed, 'batch', axis=0, tiled=True)  28.4 us
    add x8, other arithmetic, step(): current * decay_now[:, :, None, :]  24.8 us
    pmax x1, blocking collectives, shards(): top = lax.pmax(peak, 'head')  21.3 us
    psum x1, blocking collectives, shards(): summed, target = lax.psum((total * jnp.exp(peak - top), target), 'head')  17.1 us
    while x32, local copies, waits for them, and re-layouts  16.1 us
  transfers between devices with their start and end apart: 2, of which 2 were waited for; matrix products, arithmetic and copies ran while one was open for 0% of the time, Pallas kernels for 0%

commit v1 on v0

--- a/solution.py
+++ b/solution.py
@@ -120,7 +120,9 @@
         * jax.nn.sigmoid(gate)
     ).astype(jnp.bfloat16)
     partial_out = jnp.dot(gated, emission_projection, preferred_element_type=jnp.float32)
-    residual = incoming_hidden_stream.astype(jnp.float32) + lax.psum(partial_out, "head")
+    residual = incoming_hidden_stream.astype(jnp.float32) + jnp.sum(
+        lax.all_gather(partial_out, "head"), axis=0
+    )
     centered = residual - jnp.mean(residual, -1, keepdims=True)
     normed = (
         centered

time: 442 us -> 571 us (1.29)
  waiting for transfers between devices: 134 us -> 257 us
    all_gather x0 -> x1, waiting for transfers between devices: none -> 230 us  [shards(): lax.all_gather(partial_out, 'head')]
    psum x1 -> x0, waiting for transfers between devices: 105 us -> none  [shards(): lax.psum(partial_out, 'head')]
    reduce_sum x0 -> x1, other arithmetic: none -> 7.36 us  [shards(): jnp.sum(lax.all_gather(partial_out, 'head'), axis=0)]
where the time goes in v1:
time: 571 us; the launch traced here: 570 us
  waiting for transfers between devices  257 us (45%)
  matrix products  149 us (26%)
  blocking collectives  59.2 us (10%)
  other arithmetic  46.3 us (8%)
  local copies, waits for them, and re-layouts  42.7 us (7%)
  between operations  14.3 us (3%)
    all_gather x1, waiting for transfers between devices, shards(): lax.all_gather(partial_out, 'head')  230 us
    dot_general x8, matrix products, step(): jnp.einsum('bhij,bhj->bhi', current, unit_now, precision=lax.Precision.HI...  68.7 us
    dot_general x8, matrix products, step(): jnp.einsum('bhij,bhj->bhi', current, recept_now, precision=lax.Precision....  52.6 us
    all_gather x1, waiting for transfers between devices, shards(): lax.all_gather(normed, 'batch', axis=0, tiled=True)  27.3 us
    add x8, other arithmetic, step(): current * decay_now[:, :, None, :]  24.8 us
    pmax x1, blocking collectives, shards(): top = lax.pmax(peak, 'head')  21.3 us
    psum x1, blocking collectives, shards(): summed, target = lax.psum((total * jnp.exp(peak - top), target), 'head')  17.1 us
    while x32, local copies, waits for them, and re-layouts  16.1 us
  transfers between devices with their start and end apart: 2, of which 2 were waited for; matrix products, arithmetic and copies ran while one was open for 0% of the time, Pallas kernels for 0%

profile of v1, /device:TPU:0, one launch (start us, length us, event | category | flops | bytes accessed | tf_op | source)
XLA Modules:
  0.0 570.2 jit_solution(800810400440182131)
XLA Ops:
  7.2 4.9 copy.134
  27.0 185.0 %while.31 = (s32[]{:T(128)}, f32[16,8,64,64]{3,2,1,0:T(8,128)}, f32[8,16,8,64]{3,2,1,0:T(8,128)S(1)}, f32[8,16,8,64]{3,2,0,1:T(8,128)S(1)}, f32[8,16,8,64]{3,2,1...) while((s32[]{:T(128)}, f32[16,8,64,64]{3,2,1,0:T(8,128)}, ...), condition=%wide.region_2.3_spmd, body=%wide.region_1.2_spmd.sunk | while | flops 15212546 | bytes 26017968 | solution.py:42
  28.0 8.6 %fusion.40 = f32[16,8,1,64]{3,2,1,0:T(1,128)S(1)} fusion(f32[16,8,64,1]{2,3,1,0:T(1,128)S(1)} %bitcast.114, f32[16,8,64,64]{3,2,1,0:T(8,128)} %get-tuple-element.464), kind=kOutput, calls=%fused_computation.53.clone.1 | convolution fusion | flops 6291456 | bytes 2162688 | tf_op jit(solution)/shard_map/while/body/eval_jaxpr/bhij,bhj->bhi/dot_general | solution.py:33
  38.4 3.1 multiply_add_fusion.5
  43.5 6.6 %fusion.41 = f32[16,8,1,64]{3,2,1,0:T(1,128)S(1)} fusion(f32[16,8,64,64]{3,2,1,0:T(8,128)S(1)} %multiply_add_fusion.5, f32[16,8,64,1]{2,3,1,0:T(1,128)S(1)} %bitcast.113), kind=kOutput, calls=%fused_computation.54.clone.1 | convolution fusion | flops 6291456 | bytes 2162688 | tf_op jit(solution)/shard_map/while/body/eval_jaxpr/bhij,bhj->bhi/dot_general | solution.py:39
  51.1 8.6 %fusion.40 = f32[16,8,1,64]{3,2,1,0:T(1,128)S(1)} fusion(f32[16,8,64,1]{2,3,1,0:T(1,128)S(1)} %bitcast.114, f32[16,8,64,64]{3,2,1,0:T(8,128)} %get-tuple-element.464), kind=kOutput, calls=%fused_computation.53.clone.1 | convolution fusion | flops 6291456 | bytes 2162688 | tf_op jit(solution)/shard_map/while/body/eval_jaxpr/bhij,bhj->bhi/dot_general | solution.py:33
  61.5 3.1 multiply_add_fusion.5
  66.6 6.6 %fusion.41 = f32[16,8,1,64]{3,2,1,0:T(1,128)S(1)} fusion(f32[16,8,64,64]{3,2,1,0:T(8,128)S(1)} %multiply_add_fusion.5, f32[16,8,64,1]{2,3,1,0:T(1,128)S(1)} %bitcast.113), kind=kOutput, calls=%fused_computation.54.clone.1 | convolution fusion | flops 6291456 | bytes 2162688 | tf_op jit(solution)/shard_map/while/body/eval_jaxpr/bhij,bhj->bhi/dot_general | solution.py:39
  74.3 8.6 %fusion.40 = f32[16,8,1,64]{3,2,1,0:T(1,128)S(1)} fusion(f32[16,8,64,1]{2,3,1,0:T(1,128)S(1)} %bitcast.114, f32[16,8,64,64]{3,2,1,0:T(8,128)} %get-tuple-element.464), kind=kOutput, calls=%fused_computation.53.clone.1 | convolution fusion | flops 6291456 | bytes 2162688 | tf_op jit(solution)/shard_map/while/body/eval_jaxpr/bhij,bhj->bhi/dot_general | solution.py:33
  84.6 3.1 multiply_add_fusion.5
  89.8 6.6 %fusion.41 = f32[16,8,1,64]{3,2,1,0:T(1,128)S(1)} fusion(f32[16,8,64,64]{3,2,1,0:T(8,128)S(1)} %multiply_add_fusion.5, f32[16,8,64,1]{2,3,1,0:T(1,128)S(1)} %bitcast.113), kind=kOutput, calls=%fused_computation.54.clone.1 | convolution fusion | flops 6291456 | bytes 2162688 | tf_op jit(solution)/shard_map/while/body/eval_jaxpr/bhij,bhj->bhi/dot_general | solution.py:39
  97.4 8.6 %fusion.40 = f32[16,8,1,64]{3,2,1,0:T(1,128)S(1)} fusion(f32[16,8,64,1]{2,3,1,0:T(1,128)S(1)} %bitcast.114, f32[16,8,64,64]{3,2,1,0:T(8,128)} %get-tuple-element.464), kind=kOutput, calls=%fused_computation.53.clone.1 | convolution fusion | flops 6291456 | bytes 2162688 | tf_op jit(solution)/shard_map/while/body/eval_jaxpr/bhij,bhj->bhi/dot_general | solution.py:33
  112.9 6.6 %fusion.41 = f32[16,8,1,64]{3,2,1,0:T(1,128)S(1)} fusion(f32[16,8,64,64]{3,2,1,0:T(8,128)S(1)} %multiply_add_fusion.5, f32[16,8,64,1]{2,3,1,0:T(1,128)S(1)} %bitcast.113), kind=kOutput, calls=%fused_computation.54.clone.1 | convolution fusion | flops 6291456 | bytes 2162688 | tf_op jit(solution)/shard_map/while/body/eval_jaxpr/bhij,bhj->bhi/dot_general | solution.py:39
  120.5 8.6 %fusion.40 = f32[16,8,1,64]{3,2,1,0:T(1,128)S(1)} fusion(f32[16,8,64,1]{2,3,1,0:T(1,128)S(1)} %bitcast.114, f32[16,8,64,64]{3,2,1,0:T(8,128)} %get-tuple-element.464), kind=kOutput, calls=%fused_computation.53.clone.1 | convolution fusion | flops 6291456 | bytes 2162688 | tf_op jit(solution)/shard_map/while/body/eval_jaxpr/bhij,bhj->bhi/dot_general | solution.py:33
  136.0 6.6 %fusion.41 = f32[16,8,1,64]{3,2,1,0:T(1,128)S(1)} fusion(f32[16,8,64,64]{3,2,1,0:T(8,128)S(1)} %multiply_add_fusion.5, f32[16,8,64,1]{2,3,1,0:T(1,128)S(1)} %bitcast.113), kind=kOutput, calls=%fused_computation.54.clone.1 | convolution fusion | flops 6291456 | bytes 2162688 | tf_op jit(solution)/shard_map/while/body/eval_jaxpr/bhij,bhj->bhi/dot_general | solution.py:39
  143.7 8.6 %fusion.40 = f32[16,8,1,64]{3,2,1,0:T(1,128)S(1)} fusion(f32[16,8,64,1]{2,3,1,0:T(1,128)S(1)} %bitcast.114, f32[16,8,64,64]{3,2,1,0:T(8,128)} %get-tuple-element.464), kind=kOutput, calls=%fused_computation.53.clone.1 | convolution fusion | flops 6291456 | bytes 2162688 | tf_op jit(solution)/shard_map/while/body/eval_jaxpr/bhij,bhj->bhi/dot_general | solution.py:33
  159.1 6.6 %fusion.41 = f32[16,8,1,64]{3,2,1,0:T(1,128)S(1)} fusion(f32[16,8,64,64]{3,2,1,0:T(8,128)S(1)} %multiply_add_fusion.5, f32[16,8,64,1]{2,3,1,0:T(1,128)S(1)} %bitcast.113), kind=kOutput, calls=%fused_computation.54.clone.1 | convolution fusion | flops 6291456 | bytes 2162688 | tf_op jit(solution)/shard_map/while/body/eval_jaxpr/bhij,bhj->bhi/dot_general | solution.py:39
  166.8 8.6 %fusion.40 = f32[16,8,1,64]{3,2,1,0:T(1,128)S(1)} fusion(f32[16,8,64,1]{2,3,1,0:T(1,128)S(1)} %bitcast.114, f32[16,8,64,64]{3,2,1,0:T(8,128)} %get-tuple-element.464), kind=kOutput, calls=%fused_computation.53.clone.1 | convolution fusion | flops 6291456 | bytes 2162688 | tf_op jit(solution)/shard_map/while/body/eval_jaxpr/bhij,bhj->bhi/dot_general | solution.py:33
  182.3 6.6 %fusion.41 = f32[16,8,1,64]{3,2,1,0:T(1,128)S(1)} fusion(f32[16,8,64,64]{3,2,1,0:T(8,128)S(1)} %multiply_add_fusion.5, f32[16,8,64,1]{2,3,1,0:T(1,128)S(1)} %bitcast.113), kind=kOutput, calls=%fused_computation.54.clone.1 | convolution fusion | flops 6291456 | bytes 2162688 | tf_op jit(solution)/shard_map/while/body/eval_jaxpr/bhij,bhj->bhi/dot_general | solution.py:39
  189.9 8.6 %fusion.40 = f32[16,8,1,64]{3,2,1,0:T(1,128)S(1)} fusion(f32[16,8,64,1]{2,3,1,0:T(1,128)S(1)} %bitcast.114, f32[16,8,64,64]{3,2,1,0:T(8,128)} %get-tuple-element.464), kind=kOutput, calls=%fused_computation.53.clone.1 | convolution fusion | flops 6291456 | bytes 2162688 | tf_op jit(solution)/shard_map/while/body/eval_jaxpr/bhij,bhj->bhi/dot_general | solution.py:33
  205.4 6.6 %fusion.41 = f32[16,8,1,64]{3,2,1,0:T(1,128)S(1)} fusion(f32[16,8,64,64]{3,2,1,0:T(8,128)S(1)} %multiply_add_fusion.5, f32[16,8,64,1]{2,3,1,0:T(1,128)S(1)} %bitcast.113), kind=kOutput, calls=%fused_computation.54.clone.1 | convolution fusion | flops 6291456 | bytes 2162688 | tf_op jit(solution)/shard_map/while/body/eval_jaxpr/bhij,bhj->bhi/dot_general | solution.py:39
  213.8 6.3 %fusion.5 = f32[128,4096]{1,0:T(8,128)} fusion(bf16[512,4096]{1,0:T(8,128)(2,1)} %param.29, f32[128,512]{1,0:T(8,128)S(1)} %reshape.93, bf16[128,4096]{1,0:T(8,128)(2,1)S(1)} %copy-done.2, bf16[4096,512]{1,0:T(8,128)(2,1)} %param.23), kind=kOutput, calls=%fused_computation.24 | convolution fusion | flops 1074069504 | bytes 11796480 | tf_op jit(solution)/shard_map/dot_general | solution.py:122
  220.3 229.9 %all-gather.13.cloned.1.call-done = f32[1024,4096]{1,0:T(8,128)} async-done(((f32[128,4096]{1,0:T(8,128)}), f32[1024,4096]{1,0:T(8,128)}) %all-gather.13.cloned.1.call-update) | async-done | bytes 16777232 | tf_op jit(solution)/shard_map/all_gather | solution.py:124
  450.2 7.4 %reduce_sum.85 = f32[128,4096]{1,0:T(8,128)S(1)} reduce(f32[8,128,4096]{2,1,0:T(8,128)} %bitcast.110, f32[]{:T(128)} %constant.85.clone.1), dimensions={0}, to_apply=%region_6.7 | reduce | flops 3670016 | bytes 18874372 | tf_op jit(solution)/shard_map/reduce_sum | solution.py:123
  459.9 5.2 all-gather.6
  465.4 27.3 %all-gather.11.cloned.1.call-done = bf16[512,4096]{1,0:T(8,128)(2,1)} async-done(((bf16[128,4096]{1,0:T(8,128)(2,1)}), bf16[512,4096]{1,0:T(8,128)(2,1)}) %all-gather.11.cloned.1.call-update) | async-done | bytes 4194320 | tf_op jit(solution)/shard_map/all_gather | solution.py:133
  492.7 13.1 %fusion.9 = (f32[512]{0:T(512)S(1)}, f32[512,2048]{1,0:T(8,128)S(1)}) fusion(bf16[512,4096]{1,0:T(8,128)(2,1)} %all-gather.11.cloned.1.call-done, bf16[4096,2048]{1,0:T(8,128)(2,1)} %param.31), kind=kOutput, calls=%fused_computation.52 | convolution fusion | flops 8590983168 | bytes 25167872 | tf_op jit(solution)/shard_map/dot_general | solution.py:136
  507.2 5.2 all-gather.5
  512.4 5.2 all-gather.7
  517.6 5.2 all-gather.4
  523.1 21.3 %pmax.7 = f32[128]{0:T(128)S(1)} all-reduce(f32[128]{0:T(128)S(1)} %dynamic_slice.59), channel_id=1, replica_groups=mesh['head'=8,'batch'=4] {'head'}, use_global_device_ids=true, to_apply=%region_15.16 | all-reduce | flops 128 | bytes 1024 | tf_op jit(solution)/shard_map/pmax | solution.py:145
  544.6 17.1 %all-reduce = (f32[128]{0:T(128)S(1)}, f32[128]{0:T(128)S(1)}) all-reduce(f32[128]{0:T(128)S(1)} %dynamic_slice.58, f32[128]{0:T(128)S(1)} %exponential_multiply_fusion), channel_id=1, replica_groups=mesh['head'=8,'batch'=4] {'head'}, use_global_device_ids=true, to_apply=%region_14.15 | all-reduce | flops 256 | bytes 2048 | tf_op jit(solution)/shard_map/psum | solution.py:146
  (161 shorter events, 76.8 us)
Async XLA Ops:
  7.2 4.9 copy-start.2
  7.2 443.1 %all-gather.13.cloned.1.call-start = ((), (), s32[]{:S(2)}) async-start(), calls=%async_computation.1 | async-start | bytes 18874368 | tf_op jit(solution)/shard_map/all_gather | solution.py:124
  15.0 3.2 copy-start.6
  27.0 186.0 %copy-start.7 = (f32[512]{0:T(512)S(1)}, f32[512]{0:T(512)}, u32[]{:S(2)}) copy-start(f32[512]{0:T(512)} %param.27) | copy-start | bytes 6148
  27.0 11.4 %copy-start = (f32[16,8,64,64]{3,2,1,0:T(8,128)S(1)}, f32[16,8,64,64]{3,2,1,0:T(8,128)}, u32[]{:S(2)}) copy-start(f32[16,8,64,64]{3,2,1,0:T(8,128)} %get-tuple-element.464) | copy-start | bytes 6291460 | tf_op jit(solution)/shard_map/while
  41.5 2.0 copy-start.1
  50.1 11.4 %copy-start = (f32[16,8,64,64]{3,2,1,0:T(8,128)S(1)}, f32[16,8,64,64]{3,2,1,0:T(8,128)}, u32[]{:S(2)}) copy-start(f32[16,8,64,64]{3,2,1,0:T(8,128)} %get-tuple-element.464) | copy-start | bytes 6291460 | tf_op jit(solution)/shard_map/while
  64.6 2.0 copy-start.1
  73.2 11.4 %copy-start = (f32[16,8,64,64]{3,2,1,0:T(8,128)S(1)}, f32[16,8,64,64]{3,2,1,0:T(8,128)}, u32[]{:S(2)}) copy-start(f32[16,8,64,64]{3,2,1,0:T(8,128)} %get-tuple-element.464) | copy-start | bytes 6291460 | tf_op jit(solution)/shard_map/while
  87.7 2.0 copy-start.1
  96.4 11.4 %copy-start = (f32[16,8,64,64]{3,2,1,0:T(8,128)S(1)}, f32[16,8,64,64]{3,2,1,0:T(8,128)}, u32[]{:S(2)}) copy-start(f32[16,8,64,64]{3,2,1,0:T(8,128)} %get-tuple-element.464) | copy-start | bytes 6291460 | tf_op jit(solution)/shard_map/while
  110.9 2.0 copy-start.1
  119.5 11.4 %copy-start = (f32[16,8,64,64]{3,2,1,0:T(8,128)S(1)}, f32[16,8,64,64]{3,2,1,0:T(8,128)}, u32[]{:S(2)}) copy-start(f32[16,8,64,64]{3,2,1,0:T(8,128)} %get-tuple-element.464) | copy-start | bytes 6291460 | tf_op jit(solution)/shard_map/while
  134.0 2.0 copy-start.1
  142.6 11.4 %copy-start = (f32[16,8,64,64]{3,2,1,0:T(8,128)S(1)}, f32[16,8,64,64]{3,2,1,0:T(8,128)}, u32[]{:S(2)}) copy-start(f32[16,8,64,64]{3,2,1,0:T(8,128)} %get-tuple-element.464) | copy-start | bytes 6291460 | tf_op jit(solution)/shard_map/while
  157.1 2.0 copy-start.1
  165.8 11.4 %copy-start = (f32[16,8,64,64]{3,2,1,0:T(8,128)S(1)}, f32[16,8,64,64]{3,2,1,0:T(8,128)}, u32[]{:S(2)}) copy-start(f32[16,8,64,64]{3,2,1,0:T(8,128)} %get-tuple-element.464) | copy-start | bytes 6291460 | tf_op jit(solution)/shard_map/while
  180.3 2.0 copy-start.1
  188.9 11.4 %copy-start = (f32[16,8,64,64]{3,2,1,0:T(8,128)S(1)}, f32[16,8,64,64]{3,2,1,0:T(8,128)}, u32[]{:S(2)}) copy-start(f32[16,8,64,64]{3,2,1,0:T(8,128)} %get-tuple-element.464) | copy-start | bytes 6291460 | tf_op jit(solution)/shard_map/while
  203.4 2.0 copy-start.1
  220.1 272.6 %all-gather.11.cloned.1.call-start = ((), (), s32[]{:S(2)}) async-start(), calls=%async_computation | async-start | bytes 5242880 | tf_op jit(solution)/shard_map/all_gather | solution.py:133
  457.6 0.8 copy-start.3
  457.9 2.0 copy-start.4
  457.9 7.3 %copy-start.5 = (s32[16,8]{0,1:T(8,128)S(1)}, s32[16,8]{0,1:T(8,128)}, u32[]{:S(2)}) copy-start(s32[16,8]{0,1:T(8,128)} %param.33) | copy-start | bytes 1540
Sparse Core Ops, SparseCore 0:
  220.2 230.0 all-gather.12
  460.0 32.6 all-gather.10
